TPU v7x, 1024 devices: a whole 4x4x32 slice. The times are simulated.
1024 devices in a mesh: gx: 16 (over x_hi, y, core), gy: 64 (over z, x_lo).
Axes of the slice: x: 4 (x_hi: 2, x_lo: 2; x = x_hi * 2 + x_lo), y: 4, z: 32, core: 2. Of those that a mesh axis runs over, the one named last changes fastest.
Arguments:
- conserved: float32 [5, 64, 1024, 128], P(None, 'gx', 'gy'), as said below
Outputs:
- increment: float32 [5, 64, 1024, 128], P(None, 'gx', 'gy')
- blending: float32 [16, 256, 32], P('gx', 'gy')
Inputs may be any that keep to these rules, and one draw needn't show every extreme that they name: `conserved`: every node's density and pressure are positive.
All inputs are finite; a program needn't handle non-finite values. Where the computation divides by a largest or mean magnitude, that divisor is 1e-20 or more.
Results may differ from a plain program's by a relative error of at most 0.0003.
Values sent between devices are 32-bit elements; how exact they have to be, the bound alone decides.
No kernel may reach another device: no remote copies, remote signals or barrier semaphores. Data moves between devices by JAX's collectives and lax.ppermute only.
A program may use at most 32 MiB of HBM per device.

v0:
```python
import functools
import math

import jax
import jax.numpy as jnp
import numpy as np
from jax import lax
from jax.sharding import Mesh
from jax.sharding import PartitionSpec as P

GX_GY = ("gx_0", "gx_1", "gx_2", "gy_0", "gy_1")
GX = ("gx_0", "gx_1", "gx_2")
GY = ("gy_0", "gy_1")


gas_gamma = 1.4


def one_axis_at_a_time(shard, axes):
    return functools.reduce(lax.pmax, axes, shard)


def padded_2(block, sides, width):
    for axis, dim in sides:
        count = lax.axis_size(axis)
        forward = [(i, i + 1) for i in range(count - 1)]
        forward.append((count - 1, 0))
        backward = [(target, source) for source, target in forward]
        low = lax.ppermute(
            lax.slice_in_dim(block, block.shape[dim] - width, None, axis=dim), axis, forward
        )
        high = lax.ppermute(lax.slice_in_dim(block, 0, width, axis=dim), axis, backward)
        block = jnp.concatenate([low, block, high], axis=dim)
    return block


def tables():
    inverse_root = 1.0 / math.sqrt(5.0)
    points = np.array([-1.0, -inverse_root, inverse_root, 1.0])
    weights = [1.0 / 6.0, 5.0 / 6.0, 5.0 / 6.0, 1.0 / 6.0]
    barycentric = np.array(
        [
            1.0 / np.prod([points[target] - points[other] for other in range(4) if other != target])
            for target in range(4)
        ]
    )
    derivative = np.zeros((4, 4))
    for target in range(4):
        for source in range(4):
            if target != source:
                derivative[target, source] = (
                    barycentric[source] / barycentric[target] / (points[target] - points[source])
                )
    legendre = np.stack(
        [np.ones(4), points, (3.0 * points**2 - 1.0) / 2.0, (5.0 * points**3 - 3.0 * points) / 2.0],
        1,
    )
    legendre = legendre * np.sqrt(np.arange(4) + 0.5)
    weight_column = np.array(weights)[:, None]
    discrete_norms = np.sum(weight_column * legendre * legendre, 0)
    inverse = (weight_column * legendre).T / discrete_norms[:, None]
    return (weights, derivative, inverse)


def describe(conserved):
    density = conserved[0]
    velocity = conserved[1:4] / density
    pressure = (gas_gamma - 1.0) * (
        conserved[4] - 0.5 * density * jnp.sum(velocity * velocity, axis=0)
    )
    sound_speed = jnp.sqrt(gas_gamma * pressure / density)
    return (conserved, density, velocity, pressure, sound_speed)


def log_mean(left_value, right_value):
    relative = (left_value - right_value) / (left_value + right_value)
    square = relative * relative
    series = 1.0 + square / 3.0 + square * square / 5.0 + square * square * square / 7.0
    safe_relative = jnp.where(square < 0.01, 1.0, relative)
    logarithmic = jnp.log(left_value / right_value) / (2.0 * safe_relative)
    factor = jnp.where(square < 0.01, series, logarithmic)
    return (left_value + right_value) / (2.0 * factor)


def entropy_flux(left_state, right_state, normal):
    left_density, left_velocity, left_pressure = (left_state[1], left_state[2], left_state[3])
    right_density, right_velocity, right_pressure = (right_state[1], right_state[2], right_state[3])
    mean_density = log_mean(left_density, right_density)
    inverse_beta = 1.0 / log_mean(left_density / left_pressure, right_density / right_pressure)
    mean_velocity = 0.5 * (left_velocity + right_velocity)
    mean_pressure = 0.5 * (left_pressure + right_pressure)
    square_mean = 0.5 * jnp.sum(left_velocity * right_velocity, axis=0)
    mass_flux = mean_density * mean_velocity[normal]
    components = [mass_flux]
    for other in range(3):
        momentum = mass_flux * mean_velocity[other]
        if other == normal:
            momentum = momentum + mean_pressure
        components.append(momentum)
    energy_flux = mass_flux * (square_mean + inverse_beta / (gas_gamma - 1.0)) + 0.5 * (
        left_pressure * right_velocity[normal] + right_pressure * left_velocity[normal]
    )
    components.append(energy_flux)
    return jnp.stack(components)


def surface_flux(left_state, right_state, normal):
    largest = jnp.maximum(
        jnp.abs(left_state[2][normal]) + left_state[4],
        jnp.abs(right_state[2][normal]) + right_state[4],
    )
    return entropy_flux(left_state, right_state, normal) - 0.5 * largest * (
        right_state[0] - left_state[0]
    )


def accumulate(total, term):
    return term if total is None else total + term


def direction_terms(padded, dimension):
    weights, derivative, inverse = tables()
    elements = (padded.shape[dimension] - 2) // 4

    def nodes_from(start):
        return describe(
            lax.slice_in_dim(padded, start, start + 4 * (elements - 1) + 1, 4, dimension)
        )

    node_states = [nodes_from(1 + position) for position in range(4)]
    previous = nodes_from(0)
    following = nodes_from(5)
    normal = dimension - 1
    high_order = [None, None, None, None]
    for first in range(4):
        for second in range(first + 1, 4):
            pair_flux = entropy_flux(node_states[first], node_states[second], normal)
            high_order[first] = accumulate(
                high_order[first], 2.0 * float(derivative[first, second]) * pair_flux
            )
            high_order[second] = accumulate(
                high_order[second], 2.0 * float(derivative[second, first]) * pair_flux
            )
    lower_face = surface_flux(previous, node_states[0], normal)
    upper_face = surface_flux(node_states[3], following, normal)
    high_order[0] = high_order[0] - lower_face / weights[0]
    high_order[3] = high_order[3] + upper_face / weights[3]
    face_flux = (
        [lower_face]
        + [
            surface_flux(node_states[position], node_states[position + 1], normal)
            for position in range(3)
        ]
        + [upper_face]
    )
    subcell = [
        (face_flux[position + 1] - face_flux[position]) / weights[position] for position in range(4)
    ]
    layout = list(padded.shape)
    layout[dimension] = 4 * elements
    return (
        jnp.stack(high_order, dimension + 1).reshape(layout),
        jnp.stack(subcell, dimension + 1).reshape(layout),
    )


def tendency(padded, blend_weights):
    along_x = padded[:, :, 1:-1]
    along_y = padded[:, 1:-1]
    center = padded[:, 1:-1, 1:-1]
    along_z = jnp.concatenate([center[..., -1:], center, center[..., :1]], axis=3)
    high_x, subcell_x = direction_terms(along_x, 1)
    high_y, subcell_y = direction_terms(along_y, 2)
    high_z, subcell_z = direction_terms(along_z, 3)
    high_total = high_x + high_y + high_z
    subcell_total = subcell_x + subcell_y + subcell_z
    return -((1.0 - blend_weights) * high_total + blend_weights * subcell_total)


def indicator(conserved):
    weights, derivative, inverse = tables()
    state = describe(conserved)
    indicated = state[1] * state[3]
    extent = indicated.shape
    grouped = indicated.reshape(extent[0] // 4, 4, extent[1] // 4, 4, extent[2] // 4, 4)
    matrix = jnp.asarray(inverse, jnp.float32)
    coefficients = jnp.einsum(
        "ai,bj,ck,xiyjzk->abcxyz", matrix, matrix, matrix, grouped, precision=lax.Precision.HIGHEST
    )
    squares = coefficients * coefficients
    energy_all = jnp.sum(squares, axis=(0, 1, 2))
    energy_three = jnp.sum(squares[:3, :3, :3], axis=(0, 1, 2))
    energy_two = jnp.sum(squares[:2, :2, :2], axis=(0, 1, 2))
    energy = jnp.maximum(
        (energy_all - energy_three) / (energy_all + 1e-06),
        (energy_three - energy_two) / (energy_three + 1e-06),
    )
    threshold = 0.5 * 10.0 ** (-1.8 * 4.0**0.25)
    sharpness = math.log(9999.0)
    raw_blend = 1.0 / (1.0 + jnp.exp(-(sharpness / threshold) * (energy - threshold)))
    return jnp.minimum(raw_blend, 0.5)


def smooth(raw_blend, x_lower, x_upper, y_lower, y_upper):
    extended_x = jnp.concatenate([x_lower, raw_blend, x_upper], axis=0)
    extended_y = jnp.concatenate([y_lower, raw_blend, y_upper], axis=1)
    neighbours = jnp.maximum(extended_x[:-2], extended_x[2:])
    neighbours = jnp.maximum(neighbours, jnp.maximum(extended_y[:, :-2], extended_y[:, 2:]))
    neighbours = jnp.maximum(
        neighbours, jnp.maximum(jnp.roll(raw_blend, 1, 2), jnp.roll(raw_blend, -1, 2))
    )
    return jnp.maximum(raw_blend, 0.5 * neighbours)


def blend_nodes(blending):
    extent = blending.shape
    spread = jnp.broadcast_to(
        blending[:, None, :, None, :, None], (extent[0], 4, extent[1], 4, extent[2], 4)
    )
    return spread.reshape(4 * extent[0], 4 * extent[1], 4 * extent[2])


def body(conserved):
    state = describe(conserved)
    local_speed = jnp.max(jnp.sum(jnp.abs(state[2]), axis=0) + 3.0 * state[4])
    top_speed = one_axis_at_a_time(local_speed, GX_GY)
    time_step = 0.25 / top_speed
    raw_blend = indicator(conserved)
    stacked = jnp.concatenate([conserved, blend_nodes(raw_blend)[None]], axis=0)
    framed_all = padded_2(stacked, ((GX, 1), (GY, 2)), 1)
    padded = framed_all[:5]
    rims = framed_all[5]
    blending = smooth(
        raw_blend,
        rims[:1, 1:-1:4, ::4],
        rims[-1:, 1:-1:4, ::4],
        rims[1:-1:4, :1, ::4],
        rims[1:-1:4, -1:, ::4],
    )
    increment = time_step * tendency(padded, blend_nodes(blending))
    return (increment, blending)


def solution(mesh):
    split = Mesh(mesh.devices.reshape(2, 4, 2, 32, 2), ("gx_0", "gx_1", "gx_2", "gy_0", "gy_1"))
    placed = (P(None, GX, GY, None),)
    return jax.shard_map(
        body,
        mesh=split,
        in_specs=placed,
        out_specs=(P(None, GX, GY, None), P(GX, GY, None)),
        check_vma=False,
    )
```

profile of v0, /device:TPU:8, one launch (start us, length us, event | category | flops | bytes accessed | tf_op | source)
XLA Modules:
  0.0 166.6 jit_solution(10801080479933907530)
XLA Ops:
  0.6 0.8 slice_bitcast_fusion.18
  1.5 1.1 squeeze.9
  2.5 1.1 squeeze.10
  4.3 2.1 %reduce_sum.503 = f32[4,4,4,32,4]{4,3,2,1,0:T(8,128)} reshape(f32[4,16,128]{2,1,0:T(8,128)S(1)} %get-tuple-element.7) | data formatting | bytes 65536 | tf_op jit(solution)/shard_map/reduce_sum | solution.py:69
  6.3 1.6 multiply_multiply_fusion
  10.5 1.9 %collective-permute-start = (f32[6,1,16,128]{3,2,0,1:T(8,128)}, f32[6,1,16,128]{3,2,0,1:T(8,128)S(1)}, u32[]{:S(2)}, u32[]{:S(2)}) collective-permute-start(f32[6,1,16,128]{3,2,0,1:T(8,128)} %get-tuple-element.278), channel_id=1, source_target_pairs={{0,64},{64,128},{128,192},{192,256},{256,320},{320,384},{384,448},... | collective-permute-start | bytes 147464 | tf_op jit(solution)/shard_map/ppermute | solution.py:29
  12.4 3.6 %collective-permute-start.1 = (f32[6,1,16,128]{3,2,1,0:T(8,128)}, f32[6,1,16,128]{3,2,1,0:T(8,128)S(1)}, u32[]{:S(2)}, u32[]{:S(2)}) collective-permute-start(f32[6,1,16,128]{3,2,1,0:T(8,128)} %get-tuple-element.277), channel_id=1, source_target_pairs={{64,0},{128,64},{192,128},{256,192},{320,256},{384,320},{448,384},... | collective-permute-start | bytes 147464 | tf_op jit(solution)/shard_map/ppermute | solution.py:32
  16.1 1.8 %slice.912 = f32[5,4,16,32]{3,2,1,0:T(8,128)S(1)} slice(f32[5,4,16,128]{3,2,1,0:T(8,128)S(1)} %copy-done), slice={[0:5:1], [0:4:1], [0:16:1], [1:126:4]} | slice | bytes 81920 | tf_op jit(solution)/shard_map/slice | solution.py:127
  17.9 1.7 %slice.910 = f32[5,4,16,32]{3,2,1,0:T(8,128)S(1)} slice(f32[5,4,16,128]{3,2,1,0:T(8,128)S(1)} %copy-done), slice={[0:5:1], [0:4:1], [0:16:1], [0:125:4]} | slice | bytes 81920 | tf_op jit(solution)/shard_map/slice | solution.py:127
  19.7 1.8 %slice.923 = f32[5,4,16,32]{3,2,1,0:T(8,128)S(1)} slice(f32[5,4,16,128]{3,2,1,0:T(8,128)S(1)} %copy-done), slice={[0:5:1], [0:4:1], [0:16:1], [2:127:4]} | slice | bytes 81920 | tf_op jit(solution)/shard_map/slice | solution.py:127
  21.5 1.8 %slice.931 = f32[5,4,16,32]{3,2,1,0:T(8,128)S(1)} slice(f32[5,4,16,128]{3,2,1,0:T(8,128)S(1)} %copy-done), slice={[0:5:1], [0:4:1], [0:16:1], [3:128:4]} | slice | bytes 81920 | tf_op jit(solution)/shard_map/slice | solution.py:127
  23.5 1.7 %slice.941 = f32[5,4,16,32]{3,2,1,0:T(8,128)S(1)} slice(f32[5,4,16,130]{3,2,1,0:T(8,128)S(1)} %pad_maximum_fusion.3), slice={[0:5:1], [0:4:1], [0:16:1], [0:125:4]} | slice | bytes 81920 | tf_op jit(solution)/shard_map/slice | solution.py:127
  25.2 1.8 %slice.958 = f32[5,4,16,32]{3,2,1,0:T(8,128)S(1)} slice(f32[5,4,16,130]{3,2,1,0:T(8,128)S(1)} %pad_maximum_fusion.3), slice={[0:5:1], [0:4:1], [0:16:1], [5:130:4]} | slice | bytes 81920 | tf_op jit(solution)/shard_map/slice | solution.py:127
  27.2 0.8 multiply_reduce_fusion.5
  28.7 0.7 multiply_bitcast_fusion.10
  29.5 0.7 constant_dynamic-update-slice_fusion.129
  31.7 0.7 multiply_bitcast_fusion.13
  35.8 7.0 %pmax.35 = f32[]{:T(128)} all-reduce(f32[]{:T(128)} %fusion.189), channel_id=1, replica_groups=mesh['gx_0'=2,'gx_1'=4,'gx_2'=2,'gy_0'=32,'gy_1'=2] {'gx_0'}, use_global_device_ids=true, to_apply=%region_3.0 | all-reduce | flops 1 | bytes 8 | tf_op jit(solution)/shard_map/pmax | solution.py:20
  42.9 25.0 %pmax.36 = f32[]{:T(128)} all-reduce(f32[]{:T(128)} %pmax.35), channel_id=1, replica_groups=mesh['gx_0'=2,'gx_1'=4,'gx_2'=2,'gy_0'=32,'gy_1'=2] {'gx_1'}, use_global_device_ids=true, to_apply=%region_4.0 | all-reduce | flops 1 | bytes 8 | tf_op jit(solution)/shard_map/pmax | solution.py:20
  68.0 3.1 %pmax.37 = f32[]{:T(128)} all-reduce(f32[]{:T(128)} %pmax.36), channel_id=1, replica_groups=mesh['gx_0'=2,'gx_1'=4,'gx_2'=2,'gy_0'=32,'gy_1'=2] {'gx_2'}, use_global_device_ids=true, to_apply=%region_5.0 | all-reduce | flops 1 | bytes 8 | tf_op jit(solution)/shard_map/pmax | solution.py:20
  71.1 57.5 %pmax.38 = f32[]{:T(128)} all-reduce(f32[]{:T(128)} %pmax.37), channel_id=1, replica_groups=mesh['gx_0'=2,'gx_1'=4,'gx_2'=2,'gy_0'=32,'gy_1'=2] {'gy_0'}, use_global_device_ids=true, to_apply=%region_6.0 | all-reduce | flops 1 | bytes 8 | tf_op jit(solution)/shard_map/pmax | solution.py:20
  129.9 0.8 constant_dynamic-update-slice_fusion.171
  130.6 1.4 constant_dynamic-update-slice_fusion.160
  133.3 1.4 constant_dynamic-update-slice_fusion.150
  135.3 0.8 constant_dynamic-update-slice_fusion.146
  136.2 1.5 constant_dynamic-update-slice_fusion.125
  139.5 1.0 bitcast_add_fusion
  142.0 5.6 %pmax.39 = f32[]{:T(128)} all-reduce(f32[]{:T(128)} %pmax.38), channel_id=1, replica_groups=mesh['gx_0'=2,'gx_1'=4,'gx_2'=2,'gy_0'=32,'gy_1'=2] {'gy_1'}, use_global_device_ids=true, to_apply=%region_7.0 | all-reduce | flops 1 | bytes 8 | tf_op jit(solution)/shard_map/pmax | solution.py:20
  148.6 0.7 copy.243
  151.4 2.6 %collective-permute-start.3 = (f32[6,6,1,128]{3,2,1,0:T(1,128)S(1)}, f32[6,6,1,128]{3,2,1,0:T(1,128)S(1)}, u32[]{:S(2)}, u32[]{:S(2)}) collective-permute-start(f32[6,6,1,128]{3,2,1,0:T(1,128)S(1)} %get-tuple-element.262), channel_id=1, source_target_pairs={{1,0},{2,1},{3,2},{4,3},{5,4},{6,5},{7,6},{8,7},{9,8},{10,9},{11,1... | collective-permute-start | bytes 55304 | tf_op jit(solution)/shard_map/ppermute | solution.py:32
  154.0 3.4 %collective-permute-start.2 = (f32[6,6,1,128]{3,2,1,0:T(1,128)S(1)}, f32[6,6,1,128]{3,2,1,0:T(1,128)S(1)}, u32[]{:S(2)}, u32[]{:S(2)}) collective-permute-start(f32[6,6,1,128]{3,2,1,0:T(1,128)S(1)} %get-tuple-element.261), channel_id=1, source_target_pairs={{0,1},{1,2},{2,3},{3,4},{4,5},{5,6},{6,7},{7,8},{8,9},{9,10},{10,1... | collective-permute-start | bytes 55304 | tf_op jit(solution)/shard_map/ppermute | solution.py:29
  157.8 4.0 %collective-permute-done.2 = f32[6,6,1,128]{3,2,1,0:T(1,128)S(1)} collective-permute-done((f32[6,6,1,128]{3,2,1,0:T(1,128)S(1)}, f32[6,6,1,128]{3,2,1,0:T(1,128)S(1)}, u32[]{:S(2)}, u32[]{:S(2)}) %collective-permute-start.2) | collective-permute-done | bytes 18464 | tf_op jit(solution)/shard_map/ppermute | solution.py:29
  (304 shorter events, 22.3 us)
Async XLA Ops:
  0.6 3.0 %copy-start = (f32[5,4,16,128]{3,2,1,0:T(8,128)S(1)}, f32[5,4,16,128]{3,2,1,0:T(8,128)}, u32[]{:S(2)}) copy-start(f32[5,4,16,128]{3,2,1,0:T(8,128)} %param.2) | copy-start | bytes 491524
  6.3 2.1 %copy-start.23 = (f32[4,4,1,1,1]{1,0,4,3,2:T(4,128)S(1)}, f32[4,4,1,1,1]{1,0,4,3,2:T(4,128)}, u32[]{:S(2)}) copy-start(f32[4,4,1,1,1]{1,0,4,3,2:T(4,128)} %constant.323) | copy-start | bytes 196
  10.5 139.9 %collective-permute-start = (f32[6,1,16,128]{3,2,0,1:T(8,128)}, f32[6,1,16,128]{3,2,0,1:T(8,128)S(1)}, u32[]{:S(2)}, u32[]{:S(2)}) collective-permute-start(f32[6,1,16,128]{3,2,0,1:T(8,128)} %get-tuple-element.278), channel_id=1, source_target_pairs={{0,64},{64,128},{128,192},{192,256},{256,320},{320,384},{384,448},... | collective-permute-start | bytes 147464 | tf_op jit(solution)/shard_map/ppermute | solution.py:29
  12.4 138.0 %collective-permute-start.1 = (f32[6,1,16,128]{3,2,1,0:T(8,128)}, f32[6,1,16,128]{3,2,1,0:T(8,128)S(1)}, u32[]{:S(2)}, u32[]{:S(2)}) collective-permute-start(f32[6,1,16,128]{3,2,1,0:T(8,128)} %get-tuple-element.277), channel_id=1, source_target_pairs={{64,0},{128,64},{192,128},{256,192},{320,256},{384,320},{448,384},... | collective-permute-start | bytes 147464 | tf_op jit(solution)/shard_map/ppermute | solution.py:32
  30.2 0.7 copy-start.3
  31.6 2.9 %copy-start.15 = (f32[5,4,16,32]{3,2,1,0:T(8,128)}, f32[5,4,16,32]{3,2,1,0:T(8,128)S(1)}, u32[]{:S(2)}) copy-start(f32[5,4,16,32]{3,2,1,0:T(8,128)S(1)} %get-tuple-element.362) | copy-start | bytes 122884
  31.6 2.9 %copy-start.21 = (f32[4,16,128]{2,1,0:T(8,128)S(1)}, f32[4,16,128]{2,1,0:T(8,128)}, u32[]{:S(2)}) copy-start(f32[4,16,128]{2,1,0:T(8,128)} %get-tuple-element.6) | copy-start | bytes 98308
  31.7 0.7 copy-start.5
  32.4 0.7 copy-start.13
  32.5 1.4 copy-start.9
  33.1 0.7 copy-start.11
  34.5 0.7 copy-start.7
  34.5 0.7 copy-start.1
  128.6 7.5 %copy-start.16 = (f32[5,4,16,32]{3,2,1,0:T(8,128)S(1)}, f32[5,4,16,32]{3,2,1,0:T(8,128)}, u32[]{:S(2)}) copy-start(f32[5,4,16,32]{3,2,1,0:T(8,128)} %copy-done.15) | copy-start | bytes 122884
  129.2 6.8 %copy-start.10 = (f32[5,4,16,32]{3,2,1,0:T(8,128)S(1)}, f32[5,4,16,32]{3,2,1,0:T(8,128)}, u32[]{:S(2)}) copy-start(f32[5,4,16,32]{3,2,1,0:T(8,128)} %constant_dynamic-update-slice_fusion.136) | copy-start | bytes 122884
  130.6 8.9 %copy-start.20 = (f32[1,4,16,32]{3,2,1,0:T(8,128)S(1)}, f32[1,4,16,32]{3,2,1,0:T(8,128)}, u32[]{:S(2)}) copy-start(f32[1,4,16,32]{3,2,1,0:T(8,128)} %get-tuple-element.212) | copy-start | bytes 24580
  130.6 8.9 %copy-start.19 = (f32[1,4,16,32]{3,2,1,0:T(8,128)S(1)}, f32[1,4,16,32]{3,2,1,0:T(8,128)}, u32[]{:S(2)}) copy-start(f32[1,4,16,32]{3,2,1,0:T(8,128)} %get-tuple-element.267) | copy-start | bytes 24580
  132.0 7.5 %copy-start.8 = (f32[5,4,16,32,1]{3,2,1,0,4:T(8,128)S(1)}, f32[5,4,16,32,1]{3,2,1,0,4:T(8,128)}, u32[]{:S(2)}) copy-start(f32[5,4,16,32,1]{3,2,1,0,4:T(8,128)} %get-tuple-element.238) | copy-start | bytes 122884
  134.7 5.8 %copy-start.2 = (f32[5,4,16,32,1]{3,2,1,4,0:T(8,128)S(1)}, f32[5,4,16,32,1]{3,2,1,4,0:T(8,128)}, u32[]{:S(2)}) copy-start(f32[5,4,16,32,1]{3,2,1,4,0:T(8,128)} %get-tuple-element.230) | copy-start | bytes 122884
  136.2 4.4 %copy-start.18 = (f32[4,16,32]{2,1,0:T(8,128)S(1)}, f32[4,16,32]{2,1,0:T(8,128)}, u32[]{:S(2)}) copy-start(f32[4,16,32]{2,1,0:T(8,128)} %get-tuple-element.221) | copy-start | bytes 24580
  139.5 1.2 copy-start.4
  140.6 0.8 copy-start.22
  140.7 0.9 copy-start.6
  140.7 0.9 copy-start.17
  140.7 1.0 copy-start.12
  140.7 1.1 copy-start.14
  151.4 6.4 %collective-permute-start.3 = (f32[6,6,1,128]{3,2,1,0:T(1,128)S(1)}, f32[6,6,1,128]{3,2,1,0:T(1,128)S(1)}, u32[]{:S(2)}, u32[]{:S(2)}) collective-permute-start(f32[6,6,1,128]{3,2,1,0:T(1,128)S(1)} %get-tuple-element.262), channel_id=1, source_target_pairs={{1,0},{2,1},{3,2},{4,3},{5,4},{6,5},{7,6},{8,7},{9,8},{10,9},{11,1... | collective-permute-start | bytes 55304 | tf_op jit(solution)/shard_map/ppermute | solution.py:32
  154.0 7.8 %collective-permute-start.2 = (f32[6,6,1,128]{3,2,1,0:T(1,128)S(1)}, f32[6,6,1,128]{3,2,1,0:T(1,128)S(1)}, u32[]{:S(2)}, u32[]{:S(2)}) collective-permute-start(f32[6,6,1,128]{3,2,1,0:T(1,128)S(1)} %get-tuple-element.261), channel_id=1, source_target_pairs={{0,1},{1,2},{2,3},{3,4},{4,5},{5,6},{6,7},{7,8},{8,9},{9,10},{10,1... | collective-permute-start | bytes 55304 | tf_op jit(solution)/shard_map/ppermute | solution.py:29
  165.6 1.1 copy-start.24
where the time goes:
time: 167 us
  blocking collectives  98.2 us (59%)
  local copies, waits for them, and re-layouts  28.1 us (17%)
  other arithmetic  20.7 us (12%)
  starting transfers between devices  11.6 us (7%)
  waiting for transfers between devices  3.98 us (2%)
  between operations  2.91 us (2%)
    pmax x5, blocking collectives, one_axis_at_a_time(): return functools.reduce(lax.pmax, axes, shard)  98.2 us
    slice x12, local copies, waits for them, and re-layouts, nodes_from(): lax.slice_in_dim(padded, start, start + 4 * (elements - 1) + 1, 4, dimens...  11.4 us
    unnamed x99, other arithmetic  6.44 us
    unnamed x81, local copies, waits for them, and re-layouts  6.39 us
    ppermute x2, starting transfers between devices, padded_2(): lax.ppermute(lax.slice_in_dim(block, 0, width, axis=dim), axis, backward)  6.28 us
    ppermute x2, starting transfers between devices, padded_2(): lax.ppermute(lax.slice_in_dim(block, block.shape[dim] - width, None, axis...  5.29 us
    another operation x11, other arithmetic, entropy_flux(): return jnp.stack(components)  4.76 us
    ppermute x2, waiting for transfers between devices, padded_2(): lax.ppermute(lax.slice_in_dim(block, block.shape[dim] - width, None, axis...  3.97 us
  transfers between devices with their start and end apart: 4, of which 1 were waited for; matrix products, arithmetic and copies ran while one was open for 20% of the time, Pallas kernels for 0%

commit v1 on v0

v1 whole, which is shorter than its diff:
```python
import functools
import math

import jax
import jax.numpy as jnp
import numpy as np
from jax import lax
from jax.experimental import pallas as pl
from jax.experimental.pallas import tpu as pltpu
from jax.sharding import Mesh
from jax.sharding import PartitionSpec as P

GX = ("gx_0", "gx_1", "gx_2")
GY = ("gy_0", "gy_1")
EVERY = GX + GY
SIZES = (2, 4, 2, 32, 2)

VMEM_BYTES = 6 << 20

WEIGHTS = (1.0 / 6.0, 5.0 / 6.0, 5.0 / 6.0, 1.0 / 6.0)


def tables():
    inverse_root = 1.0 / math.sqrt(5.0)
    points = np.array([-1.0, -inverse_root, inverse_root, 1.0])
    barycentric = np.array(
        [
            1.0 / np.prod([points[target] - points[other] for other in range(4) if other != target])
            for target in range(4)
        ]
    )
    derivative = np.zeros((4, 4))
    for target in range(4):
        for source in range(4):
            if target != source:
                derivative[target, source] = (
                    barycentric[source] / barycentric[target] / (points[target] - points[source])
                )
    legendre = np.stack(
        [np.ones(4), points, (3.0 * points**2 - 1.0) / 2.0, (5.0 * points**3 - 3.0 * points) / 2.0],
        1,
    )
    legendre = legendre * np.sqrt(np.arange(4) + 0.5)
    weight_column = np.array(WEIGHTS)[:, None]
    discrete_norms = np.sum(weight_column * legendre * legendre, 0)
    inverse = (weight_column * legendre).T / discrete_norms[:, None]
    return derivative, inverse


DERIVATIVE, INVERSE = tables()
SPLIT = [[2.0 * WEIGHTS[k] * float(DERIVATIVE[k, j]) for j in range(4)] for k in range(4)]


def roll(value, shift, axis):
    size = value.shape[axis]
    return pltpu.roll(value, shift % size, axis)


def local_node(shape, axis):
    return lax.broadcasted_iota(jnp.int32, shape, axis) % 4


def by_node(node, values):
    out = jnp.full(node.shape, values[3], jnp.float32)
    for k in range(3):
        out = jnp.where(node == k, jnp.float32(values[k]), out)
    return out


def primitives(parts):
    density = parts[0]
    inverse = 1.0 / density
    velocity = [parts[1 + d] * inverse for d in range(3)]
    square = velocity[0] * velocity[0] + velocity[1] * velocity[1] + velocity[2] * velocity[2]
    pressure = 0.4 * (parts[4] - 0.5 * density * square)
    return density, velocity, pressure, inverse


def sound_of(pressure, inverse):
    return jnp.sqrt(1.4 * pressure * inverse)


NAMES = ("r", "u", "v", "w", "p", "c", "s", "lr", "ls", "m1", "m2", "m3", "e")


def full_state(parts):
    density, velocity, pressure, inverse = primitives(parts)
    ratio = density / pressure
    return {
        "r": density,
        "u": velocity[0],
        "v": velocity[1],
        "w": velocity[2],
        "p": pressure,
        "c": sound_of(pressure, inverse),
        "s": ratio,
        "lr": jnp.log(density),
        "ls": jnp.log(ratio),
        "m1": parts[1],
        "m2": parts[2],
        "m3": parts[3],
        "e": parts[4],
    }


def mean_parts(a, b, log_a, log_b):
    total = a + b
    gap = a - b
    relative = gap / total
    square = relative * relative
    small = square < 0.01
    series = 1.0 + square * (1.0 / 3.0 + square * (1.0 / 5.0 + square * (1.0 / 7.0)))
    top = jnp.where(small, 0.5 * total, gap)
    bottom = jnp.where(small, series, log_a - log_b)
    return top, bottom


def pair_flux(a, b, normal):
    top, bottom = mean_parts(a["r"], b["r"], a["lr"], b["lr"])
    mass = top / bottom
    top, bottom = mean_parts(a["s"], b["s"], a["ls"], b["ls"])
    inverse_beta = bottom / top
    key = "uvw"[normal]
    flux0 = mass * (0.5 * (a[key] + b[key]))
    out = [flux0]
    for other in range(3):
        name = "uvw"[other]
        term = flux0 * (0.5 * (a[name] + b[name]))
        if other == normal:
            term = term + 0.5 * (a["p"] + b["p"])
        out.append(term)
    dot = 0.5 * (a["u"] * b["u"] + a["v"] * b["v"] + a["w"] * b["w"])
    out.append(
        flux0 * (dot + 2.5 * inverse_beta) + 0.5 * (a["p"] * b[key] + b["p"] * a[key])
    )
    return out


def dissipation(a, b, normal):
    key = "uvw"[normal]
    half = 0.5 * jnp.maximum(jnp.abs(a[key]) + a["c"], jnp.abs(b[key]) + b["c"])
    return [half * (b[q] - a[q]) for q in ("r", "m1", "m2", "m3", "e")]


def speed_kernel(conserved_ref, out_ref):
    best = None
    for x in range(4):
        density, velocity, pressure, inverse = primitives([conserved_ref[q, x] for q in range(5)])
        speed = (
            jnp.abs(velocity[0])
            + jnp.abs(velocity[1])
            + jnp.abs(velocity[2])
            + 3.0 * sound_of(pressure, inverse)
        )
        best = speed if best is None else jnp.maximum(best, speed)
    row = jnp.max(best, axis=0, keepdims=True)
    out_ref[...] = jnp.broadcast_to(row[None], out_ref.shape)


def forward_kernel(in_ref, out_ref):
    row = jnp.max(in_ref[...], axis=0, keepdims=True)
    out_ref[...] = jnp.broadcast_to(row, out_ref.shape)


def transform(value, axis):
    node = local_node(value.shape, axis)
    total = None
    for offset in range(-3, 4):
        coefficients = [
            float(INVERSE[a, a + offset]) if 0 <= a + offset < 4 else 0.0 for a in range(4)
        ]
        shifted = value if offset == 0 else roll(value, -offset, axis)
        term = by_node(node, coefficients) * shifted
        total = term if total is None else total + term
    return total


def spread_sum(value, axis):
    index = lax.broadcasted_iota(jnp.int32, value.shape, axis)
    for step in (1, 2):
        other = jnp.where((index // step) % 2 == 1, roll(value, step, axis), roll(value, -step, axis))
        value = value + other
    return value


def raw_blending(layers):
    indicated = []
    for parts in layers:
        density, _, pressure, _ = primitives(parts)
        indicated.append(density * pressure)
    shape = indicated[0].shape
    node_y, node_z = local_node(shape, 0), local_node(shape, 1)
    degree = jnp.maximum(node_y, node_z)
    high = mid = low = None
    zero = jnp.zeros(shape, jnp.float32)
    for a in range(4):
        modes = sum(float(INVERSE[a, k]) * indicated[k] for k in range(4))
        modes = transform(transform(modes, 0), 1)
        square = modes * modes
        if a == 3:
            high = high + square
            continue
        top = jnp.where(degree == 3, square, zero)
        high = top if high is None else high + top
        if a == 2:
            mid = mid + jnp.where(degree < 3, square, zero)
            continue
        middle = jnp.where(degree == 2, square, zero)
        mid = middle if mid is None else mid + middle
        rest = jnp.where(degree < 2, square, zero)
        low = rest if low is None else low + rest
    high, mid, low = (spread_sum(spread_sum(v, 0), 1) for v in (high, mid, low))
    three = low + mid
    energy = jnp.maximum(high / (three + high + 1e-06), mid / (three + 1e-06))
    threshold = 0.5 * 10.0 ** (-1.8 * 4.0**0.25)
    sharpness = math.log(9999.0)
    raw = 1.0 / (1.0 + jnp.exp(-(sharpness / threshold) * (energy - threshold)))
    return jnp.minimum(raw, 0.5)


def layers_kernel(conserved_ref, _, raw_ref, xlo_ref, xhi_ref, ylo_ref, yhi_ref):
    raw = raw_blending([[conserved_ref[q, x] for q in range(5)] for x in range(4)])
    raw_ref[...] = raw
    for q in range(5):
        xlo_ref[q] = conserved_ref[q, 0]
        xhi_ref[q] = conserved_ref[q, 3]
        for x in range(4):
            ylo_ref[q, x : x + 1] = conserved_ref[q, x, 0:1]
            yhi_ref[q, x : x + 1] = conserved_ref[q, x, 15:16]
    xlo_ref[5] = raw
    xhi_ref[5] = raw
    ylo_ref[5] = jnp.broadcast_to(raw[0:1], (4, 128))
    yhi_ref[5] = jnp.broadcast_to(raw[15:16], (4, 128))


def physics_kernel(
    conserved_ref, raw_ref, xprev_ref, xnext_ref, yprev_ref, ynext_ref, out_ref, blend_ref, state_ref
):
    raw = raw_ref[...]
    shape = raw.shape
    row = lax.broadcasted_iota(jnp.int32, shape, 0)
    node_y, node_z = row % 4, local_node(shape, 1)

    before = jnp.where(row < 4, jnp.broadcast_to(yprev_ref[5, 0:1], shape), roll(raw, 4, 0))
    after = jnp.where(row >= 12, jnp.broadcast_to(ynext_ref[5, 0:1], shape), roll(raw, -4, 0))
    around = jnp.maximum(xprev_ref[5], xnext_ref[5])
    around = jnp.maximum(around, jnp.maximum(before, after))
    around = jnp.maximum(around, jnp.maximum(roll(raw, 4, 1), roll(raw, -4, 1)))
    blend = jnp.maximum(raw, 0.5 * around)
    pick_z = (
        lax.broadcasted_iota(jnp.int32, (128, 32), 0) == 4 * lax.broadcasted_iota(jnp.int32, (128, 32), 1)
    ).astype(jnp.float32)
    compact = jnp.dot(
        blend, pick_z, precision=lax.Precision.HIGHEST, preferred_element_type=jnp.float32
    )
    for element in range(4):
        blend_ref[0, element : element + 1] = compact[4 * element : 4 * element + 1]
    keep = 1.0 - blend

    for x in range(4):
        state = full_state([conserved_ref[q, x] for q in range(5)])
        for i, name in enumerate(NAMES[:9]):
            state_ref[i, x] = state[name]

    def load(x):
        state = {name: state_ref[i, x] for i, name in enumerate(NAMES[:9])}
        for i, name in enumerate(NAMES[9:]):
            state[name] = conserved_ref[1 + i, x]
        return state

    def store(x, values, first=False):
        for q in range(5):
            out_ref[q, x] = values[q] if first else out_ref[q, x] + values[q]

    y_prev = full_state([yprev_ref[q] for q in range(5)])
    y_next = full_state([ynext_ref[q] for q in range(5)])
    edge = {}
    for i, name in enumerate(NAMES[:9]):
        edge[name] = jnp.concatenate([state_ref[i, x, 0:1] for x in range(4)], axis=0)
    for i, name in enumerate(NAMES[9:]):
        edge[name] = jnp.concatenate([conserved_ref[1 + i, x, 0:1] for x in range(4)], axis=0)
    low_face = [
        f - d for f, d in zip(pair_flux(y_prev, edge, 1), dissipation(y_prev, edge, 1), strict=True)
    ]

    def along(axis, node, x, state):
        normal = axis + 1
        one = jnp.ones(shape, jnp.float32)
        step = [SPLIT[0][1], SPLIT[1][2], SPLIT[2][3], 0.0]
        inner = node < 3
        weight_f = jnp.where(inner, keep * by_node(node, step) + blend, one)
        weight_d = jnp.where(inner, blend, one)
        weight_far = keep * by_node(node, [SPLIT[0][2], SPLIT[1][3], 0.0, SPLIT[3][0]])
        next_ = {}
        for name in NAMES:
            moved = roll(state[name], -1, axis)
            if axis == 0:
                moved = jnp.where(row == 15, jnp.broadcast_to(y_next[name][x : x + 1], shape), moved)
            next_[name] = moved
        flux = pair_flux(state, next_, normal)
        loss = dissipation(state, next_, normal)
        far = {
            name: jnp.where(node == 3, roll(state[name], 3, axis), roll(state[name], -2, axis))
            for name in ("r", "u", "v", "w", "p", "s", "lr", "ls")
        }
        cross = pair_flux(state, far, normal)
        inverse_weight = by_node(node, [-1.0 / w for w in WEIGHTS])
        out = []
        for q in range(5):
            near = weight_f * flux[q] - weight_d * loss[q]
            back = roll(near, 1, axis)
            if axis == 0:
                back = jnp.where(row == 0, jnp.broadcast_to(low_face[q][x : x + 1], shape), back)
            wide = weight_far * cross[q]
            taken = jnp.where(node >= 2, roll(wide, 2, axis), jnp.where(node == 0, roll(wide, -3, axis), 0.0))
            out.append(inverse_weight * (near - back + wide - taken))
        return out

    for x in range(4):
        state = load(x)
        in_y = along(0, node_y, x, state)
        in_z = along(1, node_z, x, state)
        store(x, [a + b for a, b in zip(in_y, in_z, strict=True)], first=True)

    def gather(other):
        return full_state([other[q] for q in range(5)])

    for first in range(4):
        for second in range(first + 1, 4):
            a, b = load(first), load(second)
            flux = pair_flux(a, b, 0)
            if second == first + 1:
                weight = keep * SPLIT[first][second] + blend
                loss = dissipation(a, b, 0)
                term = [weight * f - blend * d for f, d in zip(flux, loss, strict=True)]
            else:
                weight = keep * SPLIT[first][second]
                term = [weight * f for f in flux]
            store(first, [(-1.0 / WEIGHTS[first]) * t for t in term])
            store(second, [(1.0 / WEIGHTS[second]) * t for t in term])
    a, b = gather(xprev_ref), load(0)
    flux, loss = pair_flux(a, b, 0), dissipation(a, b, 0)
    store(0, [(1.0 / WEIGHTS[0]) * (f - d) for f, d in zip(flux, loss, strict=True)])
    a, b = load(3), gather(xnext_ref)
    flux, loss = pair_flux(a, b, 0), dissipation(a, b, 0)
    store(3, [(-1.0 / WEIGHTS[3]) * (f - d) for f, d in zip(flux, loss, strict=True)])


def scale_kernel(tendency_ref, speed_ref, out_ref):
    row = jnp.max(speed_ref[...], axis=0)
    top = jnp.max(row, axis=1, keepdims=True)
    step = 0.25 / top
    for q in range(5):
        for x in range(4):
            out_ref[q, x] = tendency_ref[q, x] * step


def call(kernel, outs, *args, scratch=(), **kwargs):
    return pl.pallas_call(
        kernel,
        out_shape=[jax.ShapeDtypeStruct(shape, jnp.float32) for shape in outs],
        scratch_shapes=list(scratch),
        compiler_params=pltpu.CompilerParams(vmem_limit_bytes=VMEM_BYTES),
        **kwargs,
    )(*args)


def shift(block, axes, step):
    count = math.prod(lax.axis_size(a) for a in axes)
    return lax.ppermute(block, axes, [(i, (i + step) % count) for i in range(count)])


def z_groups():
    order = [19] + [z for z in range(32) if z != 19]
    index = np.arange(1024).reshape(SIZES).transpose(0, 1, 2, 4, 3)[..., order]
    return index.reshape(-1, 32).tolist()


def plane_groups():
    index = np.arange(1024).reshape(SIZES).transpose(3, 0, 1, 2, 4).reshape(32, 32)
    lead = int(np.ravel_multi_index((1, 2, 1, 0), (2, 4, 2, 2)))
    order = [lead] + [i for i in range(32) if i != lead]
    return index[:, order].tolist()


def exchange(rows, groups):
    return lax.all_to_all(rows, EVERY, 0, 0, axis_index_groups=groups)


def body(conserved):
    (rows,) = call(speed_kernel, [(32, 1, 128)], conserved)
    column = exchange(rows, z_groups())
    raw, xlo, xhi, ylo, yhi = call(
        layers_kernel,
        [(16, 128), (6, 16, 128), (6, 16, 128), (6, 4, 128), (6, 4, 128)],
        conserved,
        rows,
    )
    xprev = shift(xhi, GX, 1)
    xnext = shift(xlo, GX, -1)
    yprev = shift(yhi, GY, 1)
    ynext = shift(ylo, GY, -1)
    (forward,) = call(forward_kernel, [(32, 1, 128)], column)
    speeds = exchange(forward, plane_groups())
    tendency, blending = call(
        physics_kernel,
        [(5, 4, 16, 128), (1, 4, 32)],
        conserved,
        raw,
        xprev,
        xnext,
        yprev,
        ynext,
        scratch=[pltpu.VMEM((9, 4, 16, 128), jnp.float32)],
    )
    (increment,) = call(scale_kernel, [(5, 4, 16, 128)], tendency, speeds)
    return increment, blending


def solution(mesh):
    split = Mesh(mesh.devices.reshape(SIZES), EVERY)
    return jax.shard_map(
        body,
        mesh=split,
        in_specs=(P(None, GX, GY, None),),
        out_specs=(P(None, GX, GY, None), P(GX, GY, None)),
        check_vma=False,
    )
```

time: 167 us -> 66.6 us (0.40)
  the two profiles are of different devices: /device:TPU:8 before, /device:TPU:2 now
where the time goes in v1:
time: 66.6 us; the launch traced here: 66.2 us
  starting transfers between devices  55.4 us (83%)
  Pallas kernels  4.6 us (7%)
  waiting for transfers between devices  4.56 us (7%)
  local copies, waits for them, and re-layouts  0.91 us (1%)
  between operations  0.72 us (1%)
    all_to_all x2, starting transfers between devices, exchange(): return lax.all_to_all(rows, EVERY, 0, 0, axis_index_groups=groups)  39.4 us
    ppermute x4, starting transfers between devices, shift(): lax.ppermute(block, axes, [(i, (i + step) % count) for i in range(count)])  16 us
    pallas_call x5, Pallas kernels, call(): pl.pallas_call(kernel, out_shape=[jax.ShapeDtypeStruct(shape, jnp.float32...  4.6 us
    ppermute x4, waiting for transfers between devices, shift(): lax.ppermute(block, axes, [(i, (i + step) % count) for i in range(count)])  4.56 us
  transfers between devices with their start and end apart: 6, of which 1 were waited for; matrix products, arithmetic and copies ran while one was open for 0% of the time, Pallas kernels for 5%

profile of v1, /device:TPU:2, one launch (start us, length us, event | category | flops | bytes accessed | tf_op | source)
XLA Modules:
  0.0 66.2 jit_solution(9932391393577710420)
XLA Ops:
  0.6 0.0 copy-start
  0.6 0.9 %copy-done = f32[5,4,16,128]{3,2,1,0:T(8,128)S(1)} copy-done((f32[5,4,16,128]{3,2,1,0:T(8,128)S(1)}, f32[5,4,16,128]{3,2,1,0:T(8,128)}, u32[]{:S(2)}) %copy-start) | copy-done | bytes 163864
  1.5 0.0 copy-start.1
  1.5 0.7 shard_map.30._
  2.2 33.2 %all-to-all-start = ((f32[32,1,128]{2,1,0:T(1,128)}), f32[32,1,128]{2,1,0:T(1,128)S(1)}, u32[]{:S(2)}, u32[]{:S(2)}) async-start(f32[32,1,128]{2,1,0:T(1,128)} %shard_map.30._), calls=%async_computation | async-start | bytes 32768 | tf_op jit(solution)/shard_map/all_to_all | solution.py:387
  35.4 0.0 copy-done.1
  35.4 1.1 %shard_map.31 = (f32[16,128]{1,0:T(8,128)S(1)}, f32[6,16,128]{2,1,0:T(8,128)S(1)}, f32[6,16,128]{2,1,0:T(8,128)S(1)}, f32[6,4,128]{2,1,0:T(4,128)S(1)}, f32[6,4,128]{2,1,0:T(4,128)S(1)}) custom-call(f32[5,4,16,128]{3,2,1,0:T(8,128)S(1)} %copy-done.1, f32[32,1,128]{2,1,0:T(1,128)} %shard_map.30._), custom_call_target="tpu_custom_call" | custom-call | tf_op jit(solution)/shard_map/pallas_call | solution.py:359
  36.5 1.9 %collective-permute-start = (f32[6,16,128]{2,1,0:T(8,128)S(1)}, f32[6,16,128]{2,1,0:T(8,128)S(1)}, u32[]{:S(2)}, u32[]{:S(2)}) collective-permute-start(f32[6,16,128]{2,1,0:T(8,128)S(1)} %get-tuple-element.10), channel_id=1, source_target_pairs={{0,64},{64,128},{128,192},{192,256},{256,320},{320,384},{384,448},... | collective-permute-start | bytes 147464 | tf_op jit(solution)/shard_map/ppermute | solution.py:370
  38.4 7.3 %collective-permute-start.1 = (f32[6,16,128]{2,1,0:T(8,128)S(1)}, f32[6,16,128]{2,1,0:T(8,128)S(1)}, u32[]{:S(2)}, u32[]{:S(2)}) collective-permute-start(f32[6,16,128]{2,1,0:T(8,128)S(1)} %get-tuple-element.11), channel_id=1, source_target_pairs={{0,960},{64,0},{128,64},{192,128},{256,192},{320,256},{384,320},{4... | collective-permute-start | bytes 147464 | tf_op jit(solution)/shard_map/ppermute | solution.py:370
  45.7 0.0 all-to-all-done.in_ref
  45.7 0.6 shard_map.33
  46.3 6.2 %all-to-all-start.1 = ((f32[32,1,128]{2,1,0:T(1,128)}), f32[32,1,128]{2,1,0:T(1,128)S(1)}, u32[]{:S(2)}, u32[]{:S(2)}) async-start(f32[32,1,128]{2,1,0:T(1,128)} %shard_map.33), calls=%async_computation.1 | async-start | bytes 32768 | tf_op jit(solution)/shard_map/all_to_all | solution.py:387
  52.6 4.9 %collective-permute-start.2 = (f32[6,4,128]{2,1,0:T(4,128)S(1)}, f32[6,4,128]{2,1,0:T(4,128)S(1)}, u32[]{:S(2)}, u32[]{:S(2)}) collective-permute-start(f32[6,4,128]{2,1,0:T(4,128)S(1)} %get-tuple-element.12), channel_id=1, source_target_pairs={{0,1},{1,2},{2,3},{3,4},{4,5},{5,6},{6,7},{7,8},{8,9},{9,10},{10,1... | collective-permute-start | bytes 36872 | tf_op jit(solution)/shard_map/ppermute | solution.py:370
  57.5 1.9 %collective-permute-start.3 = (f32[6,4,128]{2,1,0:T(4,128)S(1)}, f32[6,4,128]{2,1,0:T(4,128)S(1)}, u32[]{:S(2)}, u32[]{:S(2)}) collective-permute-start(f32[6,4,128]{2,1,0:T(4,128)S(1)} %get-tuple-element.13), channel_id=1, source_target_pairs={{0,63},{1,0},{2,1},{3,2},{4,3},{5,4},{6,5},{7,6},{8,7},{9,8},{10,9... | collective-permute-start | bytes 36872 | tf_op jit(solution)/shard_map/ppermute | solution.py:370
  59.4 0.0 collective-permute-done.2.yprev_ref
  59.4 4.5 %collective-permute-done.3.ynext_ref = f32[6,4,128]{2,1,0:T(4,128)S(1)} collective-permute-done((f32[6,4,128]{2,1,0:T(4,128)S(1)}, f32[6,4,128]{2,1,0:T(4,128)S(1)}, u32[]{:S(2)}, u32[]{:S(2)}) %collective-permute-start.3) | collective-permute-done | bytes 12320 | tf_op jit(solution)/shard_map/ppermute | solution.py:370
  64.0 0.0 collective-permute-done.xprev_ref
  64.0 0.0 collective-permute-done.1.xnext_ref
  64.0 1.4 %shard_map.32 = (f32[5,4,16,128]{3,2,1,0:T(8,128)S(1)}, f32[1,4,32]{2,1,0:T(4,128)}) custom-call(f32[5,4,16,128]{3,2,1,0:T(8,128)S(1)} %copy-done.1, f32[16,128]{1,0:T(8,128)S(1)} %get-tuple-element.9.raw_ref, f32[6,16,128]{2,1,0:T(8,128)S(1)} %collective-permute-done.xprev_ref, f32[6,16,128]{2,1,0:T(8,128)S(1)} %collective-permute-done.1.xnext_ref, ...), custom_call_target="tpu_custom_call" | custom-call | tf_op jit(solution)/shard_map/pallas_call | solution.py:359
  65.4 0.0 all-to-all-done.1.speed_ref
  65.4 0.8 %shard_map.34 = f32[5,4,16,128]{3,2,1,0:T(8,128)} custom-call(f32[5,4,16,128]{3,2,1,0:T(8,128)S(1)} %get-tuple-element.14.tendency_ref, f32[32,1,128]{2,1,0:T(1,128)S(1)} %all-to-all-done.1.speed_ref), custom_call_target="tpu_custom_call" | custom-call | tf_op jit(solution)/shard_map/pallas_call | solution.py:359
Async XLA Ops:
  0.6 0.9 %copy-start = (f32[5,4,16,128]{3,2,1,0:T(8,128)S(1)}, f32[5,4,16,128]{3,2,1,0:T(8,128)}, u32[]{:S(2)}) copy-start(f32[5,4,16,128]{3,2,1,0:T(8,128)} %conserved_ref.5) | copy-start | bytes 491524
  1.5 33.9 %copy-start.1 = (f32[5,4,16,128]{3,2,1,0:T(8,128)S(1)}, f32[5,4,16,128]{3,2,1,0:T(8,128)}, u32[]{:S(2)}) copy-start(f32[5,4,16,128]{3,2,1,0:T(8,128)} %conserved_ref.5) | copy-start | bytes 491524
  2.2 43.5 %all-to-all-start = ((f32[32,1,128]{2,1,0:T(1,128)}), f32[32,1,128]{2,1,0:T(1,128)S(1)}, u32[]{:S(2)}, u32[]{:S(2)}) async-start(f32[32,1,128]{2,1,0:T(1,128)} %shard_map.30._), calls=%async_computation | async-start | bytes 32768 | tf_op jit(solution)/shard_map/all_to_all | solution.py:387
  36.5 27.5 %collective-permute-start = (f32[6,16,128]{2,1,0:T(8,128)S(1)}, f32[6,16,128]{2,1,0:T(8,128)S(1)}, u32[]{:S(2)}, u32[]{:S(2)}) collective-permute-start(f32[6,16,128]{2,1,0:T(8,128)S(1)} %get-tuple-element.10), channel_id=1, source_target_pairs={{0,64},{64,128},{128,192},{192,256},{256,320},{320,384},{384,448},... | collective-permute-start | bytes 147464 | tf_op jit(solution)/shard_map/ppermute | solution.py:370
  38.4 25.5 %collective-permute-start.1 = (f32[6,16,128]{2,1,0:T(8,128)S(1)}, f32[6,16,128]{2,1,0:T(8,128)S(1)}, u32[]{:S(2)}, u32[]{:S(2)}) collective-permute-start(f32[6,16,128]{2,1,0:T(8,128)S(1)} %get-tuple-element.11), channel_id=1, source_target_pairs={{0,960},{64,0},{128,64},{192,128},{256,192},{320,256},{384,320},{4... | collective-permute-start | bytes 147464 | tf_op jit(solution)/shard_map/ppermute | solution.py:370
  46.3 19.1 %all-to-all-start.1 = ((f32[32,1,128]{2,1,0:T(1,128)}), f32[32,1,128]{2,1,0:T(1,128)S(1)}, u32[]{:S(2)}, u32[]{:S(2)}) async-start(f32[32,1,128]{2,1,0:T(1,128)} %shard_map.33), calls=%async_computation.1 | async-start | bytes 32768 | tf_op jit(solution)/shard_map/all_to_all | solution.py:387
  52.6 6.8 %collective-permute-start.2 = (f32[6,4,128]{2,1,0:T(4,128)S(1)}, f32[6,4,128]{2,1,0:T(4,128)S(1)}, u32[]{:S(2)}, u32[]{:S(2)}) collective-permute-start(f32[6,4,128]{2,1,0:T(4,128)S(1)} %get-tuple-element.12), channel_id=1, source_target_pairs={{0,1},{1,2},{2,3},{3,4},{4,5},{5,6},{6,7},{7,8},{8,9},{9,10},{10,1... | collective-permute-start | bytes 36872 | tf_op jit(solution)/shard_map/ppermute | solution.py:370
  57.5 6.5 %collective-permute-start.3 = (f32[6,4,128]{2,1,0:T(4,128)S(1)}, f32[6,4,128]{2,1,0:T(4,128)S(1)}, u32[]{:S(2)}, u32[]{:S(2)}) collective-permute-start(f32[6,4,128]{2,1,0:T(4,128)S(1)} %get-tuple-element.13), channel_id=1, source_target_pairs={{0,63},{1,0},{2,1},{3,2},{4,3},{5,4},{6,5},{7,6},{8,7},{9,8},{10,9... | collective-permute-start | bytes 36872 | tf_op jit(solution)/shard_map/ppermute | solution.py:370
